TPU v7x, 256 devices: a whole 4x4x8 slice. The times are simulated.
256 devices in a mesh: dp: 32 (over z, y_hi, core), mp: 8 (over x, y_lo).
Axes of the slice: x: 4, y: 4 (y_hi: 2, y_lo: 2; y = y_hi * 2 + y_lo), z: 8, core: 2. Of those that a mesh axis runs over, the one named last changes fastest.
Arguments:
- activations: bfloat16 [16384, 28672], P('dp', 'mp'), may hold values from -200 to 200
- weight: bfloat16 [8192, 28672], P(None, ('mp', 'dp')), may hold values from -25 to 25
- thresholds: float32 [8192], P('dp'), may hold values from 0.5 to 1.5
Outputs:
- pruned: bfloat16 [8192, 28672], P('dp', 'mp')
All inputs are finite; a program needn't handle non-finite values.
Results may differ from a plain program's by a relative error of at most 0.0004.
Values may be sent and summed in bfloat16 or wider, within the bound.
A program may use at most 64 MiB of HBM per device.

v0:
```python
import jax
import jax.numpy as jnp
from jax import lax
from jax.sharding import PartitionSpec as P

IN = 28672
gate_slope = 2.0
small_eps = 1e-06


def sent_to_all(shard, axis):
    copies = jnp.broadcast_to(shard, (lax.axis_size(axis), *shard.shape))
    return lax.all_to_all(copies, axis, split_axis=0, concat_axis=0, tiled=True)


def over_copies(shard, axis):
    return sent_to_all(shard, axis).sum(axis=0)


def soft_prune(block, col_norm, row_total, limit):
    wide = block.astype(jnp.float32)
    scores = jnp.abs(wide) * col_norm[None, :]
    row_mean = row_total[:, None] / IN + small_eps
    kept_share = jnp.clip((scores / row_mean - limit[:, None]) * gate_slope + 0.5, 0.0, 1.0)
    return (wide * kept_share).astype(jnp.bfloat16)


def per_device(activations, weight, thresholds):
    partial_value = jnp.sum(jnp.square(activations.astype(jnp.float32)), axis=0)
    relaid = lax.all_to_all(weight, "dp", split_axis=0, concat_axis=1, tiled=True)
    squares = over_copies(partial_value, "dp")
    col_norm = jnp.sqrt(squares)
    row_part = jnp.sum(jnp.abs(relaid.astype(jnp.float32)) * col_norm[None, :], axis=1)
    row_total = over_copies(row_part, "mp")
    return soft_prune(relaid, col_norm, row_total, thresholds)


def solution(mesh):
    placed = (P("dp", "mp"), P(None, ("mp", "dp")), P("dp"))
    return jax.shard_map(
        per_device, mesh=mesh, in_specs=placed, out_specs=P("dp", "mp"), check_vma=False
    )
```

profile of v0, /device:TPU:16, one launch (start us, length us, event | category | flops | bytes accessed | tf_op | source)
XLA Modules:
  0.0 99.5 jit_solution(1914880998920261515)
XLA Ops:
  0.0 0.0 copy-start
  0.0 2.9 %multiply_reduce_fusion = f32[3584]{0:T(1024)S(1)} fusion(bf16[512,3584]{1,0:T(8,128)(2,1)} %param.3), kind=kLoop, calls=%fused_computation | loop fusion | flops 5501440 | bytes 3684352 | tf_op jit(solution)/shard_map/reduce_sum | solution.py:29
  2.9 1.0 %broadcast_in_dim.4 = f32[32,1,3584]{2,1,0:T(1,128)} broadcast(f32[3584]{0:T(1024)S(1)} %multiply_reduce_fusion), dimensions={2} | broadcast | bytes 473088 | tf_op jit(solution)/shard_map/broadcast_in_dim | solution.py:12
  3.9 11.6 %all-to-all-start.1 = ((f32[32,1,3584]{2,1,0:T(1,128)}), f32[32,1,3584]{2,1,0:T(1,128)S(1)}, u32[]{:S(2)}, u32[]{:S(2)}) async-start(f32[32,1,3584]{2,1,0:T(1,128)} %broadcast_in_dim.4), calls=%async_computation.1 | async-start | bytes 917504 | tf_op jit(solution)/shard_map/all_to_all | solution.py:13
  15.5 0.0 copy-done
  15.5 1.4 %copy.23 = bf16[14,32,8,256]{3,2,0,1:T(8,128)(2,1)} copy(bf16[14,32,8,256]{3,2,1,0:T(8,128)(2,1)S(1)} %bitcast.26) | data formatting | bytes 3670016 | tf_op jit(solution)/shard_map/all_to_all | solution.py:30
  16.9 0.0 copy-start.1
  16.9 14.9 %all-to-all-done.1 = f32[32,1,3584]{2,1,0:T(1,128)S(1)} async-done(((f32[32,1,3584]{2,1,0:T(1,128)}), f32[32,1,3584]{2,1,0:T(1,128)S(1)}, u32[]{:S(2)}, u32[]{:S(2)}) %all-to-all-start.1) | async-done | bytes 458784 | tf_op jit(solution)/shard_map/all_to_all | solution.py:13
  31.8 5.0 %all-to-all-start = ((bf16[32,256,112]{1,2,0:T(8,128)(2,1)}), bf16[32,256,112]{1,2,0:T(8,128)(2,1)S(1)}, u32[]{:S(2)}, u32[]{:S(2)}) async-start(bf16[32,256,112]{1,2,0:T(8,128)(2,1)} %bitcast.25), calls=%async_computation | async-start | bytes 3670016 | tf_op jit(solution)/shard_map/all_to_all | solution.py:30
  36.8 0.3 reduce_sum.37
  37.1 0.1 sqrt.12
  37.2 44.3 %all-to-all-done = bf16[32,256,112]{1,2,0:T(8,128)(2,1)S(1)} async-done(((bf16[32,256,112]{1,2,0:T(8,128)(2,1)}), bf16[32,256,112]{1,2,0:T(8,128)(2,1)S(1)}, u32[]{:S(2)}, u32[]{:S(2)}) %all-to-all-start) | async-done | bytes 1835040 | tf_op jit(solution)/shard_map/all_to_all | solution.py:30
  81.5 0.6 fusion.1
  82.0 11.0 %all_to_all.25 = f32[8,1,256]{2,1,0:T(1,128)S(1)} all-to-all(f32[8,1,256]{2,1,0:T(1,128)S(1)} %broadcast_in_dim.5), channel_id=1, replica_groups=mesh['dp'=32,'mp'=8] {'mp'}, dimensions={0} | all-to-all | bytes 16384 | tf_op jit(solution)/shard_map/all_to_all | solution.py:13
  93.1 0.0 copy-done.1
  93.1 2.6 %fusion.8 = bf16[256,3584]{0,1:T(8,128)(2,1)} fusion(bf16[32,256,112]{1,2,0:T(8,128)(2,1)S(1)} %all-to-all-done, f32[256]{0:T(256)S(1)} %copy-done.1, f32[256]{0:T(256)S(1)} %multiply_add_fusion, f32[3584]{0:T(1024)S(1)} %sqrt.11), kind=kLoop, calls=%fused_computation.12 | loop fusion | flops 9175040 | bytes 3686400 | tf_op jit(solution)/shard_map/convert_element_type | solution.py:25
  95.7 3.8 %copy.18 = bf16[256,3584]{1,0:T(8,128)(2,1)} copy(bf16[256,3584]{0,1:T(8,128)(2,1)} %fusion.8) | data formatting | bytes 3670016 | tf_op jit(solution)/shard_map/convert_element_type | solution.py:25
  (4 shorter events, 0.1 us)
Async XLA Ops:
  0.0 15.5 %copy-start = (bf16[8192,112]{0,1:T(8,128)(2,1)S(1)}, bf16[8192,112]{0,1:T(8,128)(2,1)}, u32[]{:S(2)}) copy-start(bf16[8192,112]{0,1:T(8,128)(2,1)} %param.4) | copy-start | bytes 5505028
  3.9 27.9 %all-to-all-start.1 = ((f32[32,1,3584]{2,1,0:T(1,128)}), f32[32,1,3584]{2,1,0:T(1,128)S(1)}, u32[]{:S(2)}, u32[]{:S(2)}) async-start(f32[32,1,3584]{2,1,0:T(1,128)} %broadcast_in_dim.4), calls=%async_computation.1 | async-start | bytes 917504 | tf_op jit(solution)/shard_map/all_to_all | solution.py:13
  16.9 76.2 %copy-start.1 = (f32[256]{0:T(256)S(1)}, f32[256]{0:T(256)}, u32[]{:S(2)}) copy-start(f32[256]{0:T(256)} %param.5) | copy-start | bytes 3076
  31.8 49.7 %all-to-all-start = ((bf16[32,256,112]{1,2,0:T(8,128)(2,1)}), bf16[32,256,112]{1,2,0:T(8,128)(2,1)S(1)}, u32[]{:S(2)}, u32[]{:S(2)}) async-start(bf16[32,256,112]{1,2,0:T(8,128)(2,1)} %bitcast.25), calls=%async_computation | async-start | bytes 3670016 | tf_op jit(solution)/shard_map/all_to_all | solution.py:30
where the time goes:
time: 99.9 us; the launch traced here: 99.5 us
  waiting for transfers between devices  59.2 us (59%)
  starting transfers between devices  16.6 us (17%)
  blocking collectives  11 us (11%)
  other arithmetic  6.43 us (6%)
  local copies, waits for them, and re-layouts  6.26 us (6%)
    all_to_all x1, waiting for transfers between devices, per_device(): lax.all_to_all(weight, 'dp', split_axis=0, concat_axis=1, tiled=True)  44.3 us
    all_to_all x1, waiting for transfers between devices, sent_to_all(): return lax.all_to_all(copies, axis, split_axis=0, concat_axis=0, tiled=True)  14.9 us
    all_to_all x1, starting transfers between devices, sent_to_all(): return lax.all_to_all(copies, axis, split_axis=0, concat_axis=0, tiled=True)  11.6 us
    all_to_all x1, blocking collectives, sent_to_all(): return lax.all_to_all(copies, axis, split_axis=0, concat_axis=0, tiled=True)  11 us
    all_to_all x1, starting transfers between devices, per_device(): lax.all_to_all(weight, 'dp', split_axis=0, concat_axis=1, tiled=True)  4.99 us
    convert_element_type x1, local copies, waits for them, and re-layouts, soft_prune(): return (wide * kept_share).astype(jnp.bfloat16)  3.8 us
    reduce_sum x1, other arithmetic, per_device(): partial_value = jnp.sum(jnp.square(activations.astype(jnp.float32)), axis=0)  2.92 us
    convert_element_type x1, other arithmetic, soft_prune(): return (wide * kept_share).astype(jnp.bfloat16)  2.65 us
  transfers between devices with their start and end apart: 2, of which 2 were waited for; matrix products, arithmetic and copies ran while one was open for 2% of the time, Pallas kernels for 0%

commit v1 on v0

--- a/solution.py
+++ b/solution.py
@@ -27,7 +27,10 @@
 
 def per_device(activations, weight, thresholds):
     partial_value = jnp.sum(jnp.square(activations.astype(jnp.float32)), axis=0)
-    relaid = lax.all_to_all(weight, "dp", split_axis=0, concat_axis=1, tiled=True)
+    relaid = jnp.concatenate(
+        lax.all_to_all(jnp.stack(jnp.split(weight, lax.axis_size("dp"), axis=0)), "dp", 0, 0),
+        axis=1,
+    )
     squares = over_copies(partial_value, "dp")
     col_norm = jnp.sqrt(squares)
     row_part = jnp.sum(jnp.abs(relaid.astype(jnp.float32)) * col_norm[None, :], axis=1)

time: 99.9 us -> 117 us (1.17)
  local copies, waits for them, and re-layouts: 6.26 us -> 32.5 us
  waiting for transfers between devices: 59.2 us -> 44.3 us
  starting transfers between devices: 16.6 us -> 21.4 us
    unnamed x4 -> x35, local copies, waits for them, and re-layouts: 0.01 us -> 26.7 us
    all_to_all x1, waiting for transfers between devices: 14.9 us -> 0.01 us  [sent_to_all(): return lax.all_to_all(copies, axis, split_axis=0, concat_axis=0, tiled=True)]
    all_to_all x1, starting transfers between devices: 4.99 us -> 9.78 us  [per_device(): lax.all_to_all(jnp.stack(jnp.split(weight, lax.axis_size('dp'), axis=0)),...]
    all_to_all x1 -> x0, local copies, waits for them, and re-layouts: 1.35 us -> none  [per_device(): lax.all_to_all(weight, 'dp', split_axis=0, concat_axis=1, tiled=True)]
  transfers between devices with their start and end apart: 2 -> 2, of which waited for: 2 -> 1; matrix products, arithmetic and copies ran while one was open for 2% -> 23% of each run, Pallas kernels for 0% -> 0%
where the time goes in v1:
time: 117 us; the launch traced here: 115 us
  waiting for transfers between devices  44.3 us (38%)
  local copies, waits for them, and re-layouts  32.5 us (28%)
  starting transfers between devices  21.4 us (18%)
  blocking collectives  11 us (9%)
  other arithmetic  6.29 us (5%)
    all_to_all x1, waiting for transfers between devices, per_device(): lax.all_to_all(jnp.stack(jnp.split(weight, lax.axis_size('dp'), axis=0)),...  44.3 us
    unnamed x35, local copies, waits for them, and re-layouts  26.7 us
    all_to_all x1, starting transfers between devices, sent_to_all(): return lax.all_to_all(copies, axis, split_axis=0, concat_axis=0, tiled=True)  11.6 us
    all_to_all x1, blocking collectives, sent_to_all(): return lax.all_to_all(copies, axis, split_axis=0, concat_axis=0, tiled=True)  11 us
    all_to_all x1, starting transfers between devices, per_device(): lax.all_to_all(jnp.stack(jnp.split(weight, lax.axis_size('dp'), axis=0)),...  9.78 us
    convert_element_type x1, local copies, waits for them, and re-layouts, soft_prune(): return (wide * kept_share).astype(jnp.bfloat16)  3.8 us
    reduce_sum x1, other arithmetic, per_device(): partial_value = jnp.sum(jnp.square(activations.astype(jnp.float32)), axis=0)  2.79 us
    convert_element_type x1, other arithmetic, soft_prune(): return (wide * kept_share).astype(jnp.bfloat16)  2.65 us
  transfers between devices with their start and end apart: 2, of which 1 were waited for; matrix products, arithmetic and copies ran while one was open for 23% of the time, Pallas kernels for 0%

profile of v1, /device:TPU:16, one launch (start us, length us, event | category | flops | bytes accessed | tf_op | source)
XLA Modules:
  0.0 115.5 jit_solution(5318130908527269115)
XLA Ops:
  0.0 2.8 %multiply_reduce_fusion = f32[3584]{0:T(1024)S(1)} fusion(bf16[512,3584]{1,0:T(8,128)(2,1)} %param.3), kind=kLoop, calls=%fused_computation | loop fusion | flops 5501440 | bytes 3684352 | tf_op jit(solution)/shard_map/reduce_sum | solution.py:29
  2.8 1.0 broadcast_in_dim.4
  3.8 11.6 %all-to-all-start.1 = ((f32[32,1,3584]{2,1,0:T(1,128)}), f32[32,1,3584]{2,1,0:T(1,128)S(1)}, u32[]{:S(2)}, u32[]{:S(2)}) async-start(f32[32,1,3584]{2,1,0:T(1,128)} %broadcast_in_dim.4), calls=%async_computation.1 | async-start | bytes 917504 | tf_op jit(solution)/shard_map/all_to_all | solution.py:13
  15.4 0.8 constant_dynamic-update-slice_fusion.31
  16.2 0.8 constant_dynamic-update-slice_fusion.30
  17.0 0.8 constant_dynamic-update-slice_fusion.29
  17.9 0.8 constant_dynamic-update-slice_fusion.28
  18.7 0.8 constant_dynamic-update-slice_fusion.27
  19.5 0.8 constant_dynamic-update-slice_fusion.26
  20.3 0.8 constant_dynamic-update-slice_fusion.25
  21.2 0.8 constant_dynamic-update-slice_fusion.24
  22.0 0.8 constant_dynamic-update-slice_fusion.23
  22.8 0.8 constant_dynamic-update-slice_fusion.22
  23.6 0.8 constant_dynamic-update-slice_fusion.21
  24.4 0.8 constant_dynamic-update-slice_fusion.20
  25.3 0.8 constant_dynamic-update-slice_fusion.19
  26.1 0.8 constant_dynamic-update-slice_fusion.18
  26.9 0.8 constant_dynamic-update-slice_fusion.17
  27.7 0.8 constant_dynamic-update-slice_fusion.16
  28.6 0.8 constant_dynamic-update-slice_fusion.15
  29.4 0.8 constant_dynamic-update-slice_fusion.14
  30.2 0.8 constant_dynamic-update-slice_fusion.13
  31.0 0.8 constant_dynamic-update-slice_fusion.12
  31.9 0.8 constant_dynamic-update-slice_fusion.11
  32.7 0.8 constant_dynamic-update-slice_fusion.10
  33.5 0.8 constant_dynamic-update-slice_fusion.9
  34.3 0.8 constant_dynamic-update-slice_fusion.8
  35.1 0.8 constant_dynamic-update-slice_fusion.7
  36.0 0.8 constant_dynamic-update-slice_fusion.6
  36.8 0.8 constant_dynamic-update-slice_fusion.5
  37.6 0.8 constant_dynamic-update-slice_fusion.4
  38.4 0.8 constant_dynamic-update-slice_fusion.3
  39.3 0.8 constant_dynamic-update-slice_fusion.2
  40.1 0.8 constant_dynamic-update-slice_fusion.1
  40.9 0.8 constant_dynamic-update-slice_fusion
  41.7 0.0 copy-start
  41.7 1.2 %copy-done = bf16[32,256,112]{1,2,0:T(8,128)(2,1)} copy-done((bf16[32,256,112]{1,2,0:T(8,128)(2,1)}, bf16[32,256,112]{1,2,0:T(8,128)(2,1)S(1)}, u32[]{:S(2)}) %copy-start) | copy-done | bytes 1835032
  43.0 0.0 all-to-all-done.1
  43.0 9.8 %all-to-all-start = ((bf16[32,256,112]{1,2,0:T(8,128)(2,1)}), bf16[32,256,112]{1,2,0:T(8,128)(2,1)S(1)}, u32[]{:S(2)}, u32[]{:S(2)}) async-start(bf16[32,256,112]{1,2,0:T(8,128)(2,1)} %copy-done), calls=%async_computation | async-start | bytes 3670016 | tf_op jit(solution)/shard_map/all_to_all | solution.py:31
  52.7 0.0 copy-start.1
  52.8 0.3 reduce_sum.37
  53.1 0.1 sqrt.12
  53.1 44.3 %all-to-all-done = bf16[32,256,112]{1,2,0:T(8,128)(2,1)S(1)} async-done(((bf16[32,256,112]{1,2,0:T(8,128)(2,1)}), bf16[32,256,112]{1,2,0:T(8,128)(2,1)S(1)}, u32[]{:S(2)}, u32[]{:S(2)}) %all-to-all-start) | async-done | bytes 1835040 | tf_op jit(solution)/shard_map/all_to_all | solution.py:31
  97.4 0.6 fusion.1
  98.0 11.0 %all_to_all.17 = f32[8,1,256]{2,1,0:T(1,128)S(1)} all-to-all(f32[8,1,256]{2,1,0:T(1,128)S(1)} %broadcast_in_dim.5), channel_id=1, replica_groups=mesh['dp'=32,'mp'=8] {'mp'}, dimensions={0} | all-to-all | bytes 16384 | tf_op jit(solution)/shard_map/all_to_all | solution.py:13
  109.0 0.0 copy-done.1
  109.0 2.6 %fusion.8 = bf16[256,3584]{0,1:T(8,128)(2,1)} fusion(bf16[32,256,112]{1,2,0:T(8,128)(2,1)S(1)} %all-to-all-done, f32[256]{0:T(256)S(1)} %copy-done.1, f32[256]{0:T(256)S(1)} %multiply_add_fusion, f32[3584]{0:T(1024)S(1)} %sqrt.11), kind=kLoop, calls=%fused_computation.12 | loop fusion | flops 9175040 | bytes 3686400 | tf_op jit(solution)/shard_map/convert_element_type | solution.py:25
  111.7 3.8 %copy.9 = bf16[256,3584]{1,0:T(8,128)(2,1)} copy(bf16[256,3584]{0,1:T(8,128)(2,1)} %fusion.8) | data formatting | bytes 3670016 | tf_op jit(solution)/shard_map/convert_element_type | solution.py:25
  (4 shorter events, 0.1 us)
Async XLA Ops:
  3.8 39.2 %all-to-all-start.1 = ((f32[32,1,3584]{2,1,0:T(1,128)}), f32[32,1,3584]{2,1,0:T(1,128)S(1)}, u32[]{:S(2)}, u32[]{:S(2)}) async-start(f32[32,1,3584]{2,1,0:T(1,128)} %broadcast_in_dim.4), calls=%async_computation.1 | async-start | bytes 917504 | tf_op jit(solution)/shard_map/all_to_all | solution.py:13
  41.7 1.2 %copy-start = (bf16[32,256,112]{1,2,0:T(8,128)(2,1)}, bf16[32,256,112]{1,2,0:T(8,128)(2,1)S(1)}, u32[]{:S(2)}) copy-start(bf16[32,256,112]{1,2,0:T(8,128)(2,1)S(1)} %constant_dynamic-update-slice_fusion) | copy-start | bytes 5505028
  43.0 54.5 %all-to-all-start = ((bf16[32,256,112]{1,2,0:T(8,128)(2,1)}), bf16[32,256,112]{1,2,0:T(8,128)(2,1)S(1)}, u32[]{:S(2)}, u32[]{:S(2)}) async-start(bf16[32,256,112]{1,2,0:T(8,128)(2,1)} %copy-done), calls=%async_computation | async-start | bytes 3670016 | tf_op jit(solution)/shard_map/all_to_all | solution.py:31
  52.7 56.3 %copy-start.1 = (f32[256]{0:T(256)S(1)}, f32[256]{0:T(256)}, u32[]{:S(2)}) copy-start(f32[256]{0:T(256)} %param.5) | copy-start | bytes 3076
